TPU v7x, 32 devices: a whole 2x2x4 slice. The times are simulated.
32 devices in a mesh: groups: 2 (over x), ep: 8 (over z, y), tp: 2 (over core).
Axes of the slice: x: 2, y: 2, z: 4, core: 2. Of those that a mesh axis runs over, the one named last changes fastest.
Arguments:
- hidden: bfloat16 [256, 3584], P(('groups', 'ep'), 'tp'), parts along dimension 0, may hold values from -6 to 6
- routes: int32 [256, 4], P(('groups', 'ep')), parts along dimension 0, may hold values from 0 to 7, as said below
- router_weight: bfloat16 [3584, 8], P('tp'), may hold values from -0.1875 to 0.1875
- gate_weight: bfloat16 [8, 3584, 1024], P('ep', None, 'tp'), may hold values from -0.09375 to 0.09375
- up_weight: bfloat16 [8, 3584, 1024], P('ep', None, 'tp'), may hold values from -0.09375 to 0.09375
- down_weight: bfloat16 [8, 1024, 3584], P('ep', 'tp'), may hold values from -0.1875 to 0.1875
- q_latent: bfloat16 [64, 64, 512], P(('groups', 'ep'), 'tp'), parts along dimension 0, may hold values from -48 to 48
- q_rope: bfloat16 [64, 64, 64], P(('groups', 'ep'), 'tp'), parts along dimension 0, may hold values from -48 to 48
- cache_latent: bfloat16 [64, 256, 512], P(('groups', 'ep')), parts along dimension 0, may hold values from -4 to 4
- cache_rope: bfloat16 [64, 64, 256], P(('groups', 'ep')), parts along dimension 0, may hold values from -4 to 4
- lengths: int32 [64], P(('groups', 'ep')), parts along dimension 0, may hold values from 16 to 256, as said below
Outputs:
- moe_out: bfloat16 [256, 3584], P(('groups', 'ep'), 'tp'), parts along dimension 0
- attn_latent: bfloat16 [64, 64, 512], P(('groups', 'ep'), 'tp'), parts along dimension 0
There are 2 independent parts, one for each index of `groups`. A program takes and returns all parts, laid end to end along the dimension named above; an argument that names none is the same for every part. Nothing has to cross between parts.
Inputs may be any that keep to these rules, and one draw needn't show every extreme that they name: `routes`: each row names 4 different experts; in each aligned block of 16 rows (the rows of one index of ep) no expert is named more than 16 times, and one expert, the same in every block, is named exactly 16 times in each block. `lengths`: one sequence has 256 live positions and one has 16.
All inputs are finite; a program needn't handle non-finite values.
Results may differ from a plain program's by a relative error of at most 0.0085.
Values may be sent and summed in bfloat16 or wider, within the bound.
A program may use at most 128 MiB of HBM per device.

v0:
```python
import jax
import jax.numpy as jnp
from jax import lax
from jax.sharding import PartitionSpec as P

softmax_scale = 192.0 ** (-0.5)
routed_scale = 2.5


def local(
    hidden,
    routes,
    router_weight,
    gate_weight,
    up_weight,
    down_weight,
    q_latent,
    q_rope,
    cache_latent,
    cache_rope,
    lengths,
):
    token_count, top_count = routes.shape
    expert_count = lax.axis_size("ep")
    capacity = min(token_count, 4 * token_count * top_count // expert_count)
    partial_logits = jnp.dot(hidden, router_weight, preferred_element_type=jnp.float32)
    logits = lax.psum(partial_logits, "tp")
    affinity = jax.nn.sigmoid(logits)
    expert_iota = jnp.arange(expert_count, dtype=jnp.int32)
    chosen_mask = routes[:, :, None] == expert_iota[None, None, :]
    chosen = jnp.sum(jnp.where(chosen_mask, affinity[:, None, :], 0.0), axis=2)
    gates = routed_scale * chosen / jnp.sum(chosen, axis=1, keepdims=True)
    flat_mask = chosen_mask.reshape(token_count * top_count, expert_count).astype(jnp.int32)
    earlier = jnp.cumsum(flat_mask, axis=0) - flat_mask
    within = jnp.sum(flat_mask * earlier, axis=1).reshape(token_count, top_count)
    slot_index = routes * capacity + within
    slot_iota = jnp.arange(expert_count * capacity, dtype=jnp.int32)
    placing = jnp.sum(
        (slot_index[None, :, :] == slot_iota[:, None, None]).astype(jnp.int32), axis=2
    )
    placing = placing.astype(jnp.bfloat16)
    outgoing = jnp.dot(placing, hidden, preferred_element_type=jnp.float32).astype(jnp.bfloat16)
    outgoing = outgoing.reshape(expert_count, capacity, hidden.shape[1])
    received = lax.all_to_all(outgoing, "ep", split_axis=0, concat_axis=0, tiled=True)
    received = lax.all_gather(received, "tp", axis=2, tiled=True)
    source_count, slot_count, feature_count = received.shape
    flat_rows = received.reshape(source_count * slot_count, feature_count)
    gate_part = jnp.dot(flat_rows, gate_weight[0], preferred_element_type=jnp.float32)
    up_part = jnp.dot(flat_rows, up_weight[0], preferred_element_type=jnp.float32)
    active = (jax.nn.silu(gate_part) * up_part).astype(jnp.bfloat16)
    partial_out = jnp.dot(active, down_weight[0], preferred_element_type=jnp.float32)
    summed = lax.psum_scatter(partial_out, "tp", scatter_dimension=1, tiled=True).astype(
        jnp.bfloat16
    )
    summed = summed.reshape(source_count, slot_count, summed.shape[1])
    returned = lax.all_to_all(summed, "ep", split_axis=0, concat_axis=0, tiled=True)
    scores = jnp.einsum("bhl,bjl->bhj", q_latent, cache_latent, preferred_element_type=jnp.float32)
    scores = scores + jnp.einsum(
        "bhr,brj->bhj", q_rope, cache_rope, preferred_element_type=jnp.float32
    )
    scores = scores * softmax_scale
    position = jnp.arange(cache_latent.shape[1], dtype=jnp.int32)
    live = position[None, None, :] < lengths[:, None, None]
    scores = jnp.where(live, scores, -jnp.inf)
    highest = jnp.max(scores, axis=2, keepdims=True)
    expo = jnp.where(live, jnp.exp(scores - highest), 0.0)
    attn_probs = (expo / jnp.sum(expo, axis=2, keepdims=True)).astype(jnp.bfloat16)
    attn_latent = jnp.einsum(
        "bhj,bjl->bhl", attn_probs, cache_latent, preferred_element_type=jnp.float32
    )
    attn_latent = attn_latent.astype(jnp.bfloat16)
    returned_flat = returned.reshape(expert_count * capacity, returned.shape[2])
    picked = jnp.take(returned_flat, slot_index.reshape(-1), axis=0).reshape(
        token_count, top_count, returned.shape[2]
    )
    moe_out = jnp.sum(gates[:, :, None] * picked.astype(jnp.float32), axis=1).astype(jnp.bfloat16)
    return (moe_out, attn_latent)


def solution(mesh):
    return jax.shard_map(
        local,
        mesh=mesh,
        in_specs=(
            P(("groups", "ep"), "tp"),
            P(("groups", "ep"), None),
            P("tp", None),
            P("ep", None, "tp"),
            P("ep", None, "tp"),
            P("ep", "tp", None),
            P(("groups", "ep"), "tp", None),
            P(("groups", "ep"), "tp", None),
            P(("groups", "ep"), None, None),
            P(("groups", "ep"), None, None),
            P(("groups", "ep")),
        ),
        out_specs=(P(("groups", "ep"), "tp"), P(("groups", "ep"), "tp", None)),
        check_vma=False,
    )
```

profile of v0, /device:TPU:0, one launch (start us, length us, event | category | flops | bytes accessed | tf_op | source)
XLA Modules:
  0.0 79.6 jit_solution(17327252212873637987)
XLA Ops:
  7.2 0.0 copy-start
  7.2 0.0 reduce-scatter.2.cloned.1.call-start
  7.2 0.8 %copy.22 = s32[16,4]{1,0:T(8,128)S(1)} copy(s32[16,4]{0,1:T(4,128)} %param.12) | data formatting | bytes 512 | tf_op args[1]
  8.1 0.1 eq.38
  8.2 0.1 fusion.27
  8.2 0.1 reduce_window_sum.11
  8.3 0.2 select_reduce_fusion
  8.5 0.1 reshape.109
  8.6 0.1 copy.24
  8.7 0.1 convert_reduce_fusion
  8.8 1.1 %convolution_convert_fusion = bf16[128,1792]{1,0:T(8,128)(2,1)S(1)} fusion(bf16[16,1792]{1,0:T(8,128)(2,1)} %param.11, s32[128,16]{0,1:T(8,128)S(1)} %convert_reduce_fusion), kind=kOutput, calls=%fused_computation.8 | convolution fusion | flops 7571456 | bytes 524288 | tf_op jit(solution)/shard_map/dot_general | solution.py:42
  9.9 20.3 %all_to_all.10 = bf16[8,16,1792]{2,1,0:T(8,128)(2,1)S(1)} all-to-all(bf16[8,16,1792]{2,1,0:T(8,128)(2,1)S(1)} %bitcast.36), channel_id=1, replica_groups=mesh['groups'=2,'ep'=8,'tp'=2] {'ep'}, dimensions={0} | all-to-all | bytes 917504 | tf_op jit(solution)/shard_map/all_to_all | solution.py:44
  30.2 2.5 %all_gather.3 = bf16[8,16,3584]{2,1,0:T(8,128)(2,1)S(1)} all-gather(bf16[8,16,1792]{2,1,0:T(8,128)(2,1)S(1)} %all_to_all.10), channel_id=1, replica_groups=mesh['groups'=2,'ep'=8,'tp'=2] {'tp'}, dimensions={2}, use_global_device_ids=true | all-gather | bytes 1376256 | tf_op jit(solution)/shard_map/all_gather | solution.py:45
  32.7 2.7 %fusion.5 = f32[128,512]{1,0:T(8,128)S(1)} fusion(bf16[128,3584]{1,0:T(8,128)(2,1)S(1)} %bitcast.34, bf16[1,3584,512]{2,1,0:T(8,128)(2,1)} %param.14), kind=kOutput, calls=%fused_computation.6 | convolution fusion | flops 469762048 | bytes 4849664 | tf_op jit(solution)/shard_map/dot_general | solution.py:48
  35.4 0.0 copy-start.1
  35.4 0.0 copy-start.5
  35.4 0.0 copy-start.6
  35.4 0.0 copy-start.2
  35.4 5.7 %fusion.1 = f32[128,3584]{1,0:T(8,128)} fusion(bf16[1,512,3584]{2,1,0:T(8,128)(2,1)} %param.16, bf16[128,3584]{1,0:T(8,128)(2,1)S(1)} %bitcast.35, bf16[1,3584,512]{2,1,0:T(8,128)(2,1)} %param.15, f32[128,512]{1,0:T(8,128)S(1)} %fusion.5), kind=kOutput, calls=%fused_computation.2 | convolution fusion | flops 939917312 | bytes 10354688 | tf_op jit(solution)/shard_map/dot_general | solution.py:51
  41.1 0.0 copy-start.7
  41.1 0.0 copy-start.3
  41.1 0.0 copy-start.4
  41.1 0.0 reduce-scatter.2.cloned.1.call-update
  41.1 0.1 reshape.114
  41.2 0.0 copy-done.1
  41.2 0.0 copy-done.5
  41.2 0.1 fusion.34
  41.3 2.5 %psum.7 = f32[16,8]{0,1:T(8,128)S(1)} all-reduce(f32[16,8]{0,1:T(8,128)S(1)} %fusion.34), channel_id=1, replica_groups=mesh['groups'=2,'ep'=8,'tp'=2] {'tp'}, use_global_device_ids=true, to_apply=%region_0.0 | all-reduce | flops 128 | bytes 1024 | tf_op jit(solution)/shard_map/psum | solution.py:27
  43.8 0.0 copy-done.6
  43.9 0.1 copy.21
  44.0 0.0 copy-done
  44.0 0.0 copy-done.2
  44.0 0.4 fusion.35
  44.4 5.2 %reduce-scatter.2.cloned.1.call-done = f32[128,1792]{1,0:T(8,128)} async-done(((f32[128,3584]{1,0:T(8,128)}), f32[128,1792]{1,0:T(8,128)}) %reduce-scatter.2.cloned.1.call-update) | async-done | bytes 917520 | tf_op jit(solution)/shard_map/reduce_scatter | solution.py:52
  49.6 2.0 %convert_element_type.35 = bf16[128,1792]{1,0:T(8,128)(2,1)} convert(f32[128,1792]{1,0:T(8,128)} %reduce-scatter.2.cloned.1.call-done) | non-fusion elementwise | flops 229376 | bytes 1376256 | tf_op jit(solution)/shard_map/convert_element_type | solution.py:52
  51.6 5.9 %all-to-all-start.1 = ((bf16[8,16,1792]{2,1,0:T(8,128)(2,1)}), bf16[8,16,1792]{2,1,0:T(8,128)(2,1)S(1)}, u32[]{:S(2)}, u32[]{:S(2)}) async-start(bf16[8,16,1792]{2,1,0:T(8,128)(2,1)} %bitcast.5), calls=%async_computation.2 | async-start | bytes 917504 | tf_op jit(solution)/shard_map/all_to_all | solution.py:56
  57.4 0.0 copy-done.7
  57.4 0.1 iota_compare_fusion.3
  57.5 0.0 copy-done.3
  57.5 0.0 copy-done.4
  57.5 0.2 fusion.17
  57.7 0.2 fusion.33
  57.9 1.0 %convolution_convert_fusion.1 = bf16[4,32,512]{2,1,0:T(8,128)(2,1)} fusion(bf16[4,256,512]{2,1,0:T(8,128)(2,1)S(1)} %copy-done, f32[4,32]{1,0:T(4,128)S(1)} %fusion.33, f32[4,32,256]{2,1,0:T(8,128)S(1)} %fusion.17, pred[4,256]{1,0:T(4,128)(4,1)S(1)} %iota_compare_fusion.3), kind=kOutput, calls=%fused_computation.11 | convolution fusion | flops 33751424 | bytes 1312256 | tf_op jit(solution)/shard_map/bhj,bjl->bhl/dot_general | solution.py:68
  58.8 12.0 %all-to-all-done.1 = bf16[8,16,1792]{2,1,0:T(8,128)(2,1)S(1)} async-done(((bf16[8,16,1792]{2,1,0:T(8,128)(2,1)}), bf16[8,16,1792]{2,1,0:T(8,128)(2,1)S(1)}, u32[]{:S(2)}, u32[]{:S(2)}) %all-to-all-start.1) | async-done | bytes 458784 | tf_op jit(solution)/shard_map/all_to_all | solution.py:56
  70.8 0.7 gather_fusion
  71.6 0.1 gather.7
  71.7 1.1 %multiply_reduce_fusion = bf16[16,1792]{1,0:T(8,128)(2,1)} fusion(bf16[16,4,1792]{2,1,0:T(4,128)(2,1)S(1)} %gather.7, f32[16,4]{1,0:T(8,128)S(1)} %copy.21, pred[16,4]{1,0:T(8,128)(4,1)S(1)} %get-tuple-element.4), kind=kLoop, calls=%fused_computation.18 | loop fusion | flops 430080 | bytes 287040 | tf_op jit(solution)/shard_map/reduce_sum | solution.py:76
  (6 shorter events, 0.1 us)
Async XLA Ops:
  7.2 36.8 %copy-start = (bf16[4,256,512]{2,1,0:T(8,128)(2,1)S(1)}, bf16[4,256,512]{2,1,0:T(8,128)(2,1)}, u32[]{:S(2)}) copy-start(bf16[4,256,512]{2,1,0:T(8,128)(2,1)} %param.19) | copy-start | bytes 3145732
  7.2 42.4 %reduce-scatter.2.cloned.1.call-start = ((), (), s32[]{:S(2)}) async-start(), calls=%async_computation.3 | async-start | bytes 2752512 | tf_op jit(solution)/shard_map/reduce_scatter | solution.py:52
  35.4 5.9 %copy-start.1 = (bf16[16,1792]{1,0:T(8,128)(2,1)S(1)}, bf16[16,1792]{1,0:T(8,128)(2,1)}, u32[]{:S(2)}) copy-start(bf16[16,1792]{1,0:T(8,128)(2,1)} %param.11) | copy-start | bytes 172036
  35.4 5.9 %copy-start.5 = (bf16[1792,8]{0,1:T(8,128)(2,1)S(1)}, bf16[1792,8]{0,1:T(8,128)(2,1)}, u32[]{:S(2)}) copy-start(bf16[1792,8]{0,1:T(8,128)(2,1)} %param.13) | copy-start | bytes 86020
  35.4 8.4 %copy-start.6 = (s32[16,4]{0,1:T(4,128)S(1)}, s32[16,4]{0,1:T(4,128)}, u32[]{:S(2)}) copy-start(s32[16,4]{0,1:T(4,128)} %param.12) | copy-start | bytes 772
  35.4 8.6 %copy-start.2 = (bf16[4,32,512]{2,1,0:T(8,128)(2,1)S(1)}, bf16[4,32,512]{2,1,0:T(8,128)(2,1)}, u32[]{:S(2)}) copy-start(bf16[4,32,512]{2,1,0:T(8,128)(2,1)} %param.17) | copy-start | bytes 393220
  41.1 16.3 %copy-start.7 = (s32[4]{0:T(128)S(1)}, s32[4]{0:T(128)}, u32[]{:S(2)}) copy-start(s32[4]{0:T(128)} %param.21) | copy-start | bytes 52
  41.1 16.4 %copy-start.3 = (bf16[4,64,256]{2,1,0:T(8,128)(2,1)S(1)}, bf16[4,64,256]{2,1,0:T(8,128)(2,1)}, u32[]{:S(2)}) copy-start(bf16[4,64,256]{2,1,0:T(8,128)(2,1)} %param.20) | copy-start | bytes 393220
  41.1 16.4 %copy-start.4 = (bf16[4,32,64]{2,1,0:T(8,128)(2,1)S(1)}, bf16[4,32,64]{2,1,0:T(8,128)(2,1)}, u32[]{:S(2)}) copy-start(bf16[4,32,64]{2,1,0:T(8,128)(2,1)} %param.18) | copy-start | bytes 49156
  51.6 19.3 %all-to-all-start.1 = ((bf16[8,16,1792]{2,1,0:T(8,128)(2,1)}), bf16[8,16,1792]{2,1,0:T(8,128)(2,1)S(1)}, u32[]{:S(2)}, u32[]{:S(2)}) async-start(bf16[8,16,1792]{2,1,0:T(8,128)(2,1)} %bitcast.5), calls=%async_computation.2 | async-start | bytes 917504 | tf_op jit(solution)/shard_map/all_to_all | solution.py:56
Sparse Core Ops, SparseCore 0:
  41.2 8.2 reduce-scatter.1
where the time goes:
time: 80 us; the launch traced here: 79.6 us
  blocking collectives  25.2 us (32%)
  waiting for transfers between devices  17.2 us (22%)
  between operations  14.2 us (18%)
  matrix products  11.2 us (14%)
  starting transfers between devices  5.91 us (7%)
  other arithmetic  3.88 us (5%)
  local copies, waits for them, and re-layouts  2.09 us (3%)
    all_to_all x1, blocking collectives, local(): lax.all_to_all(outgoing, 'ep', split_axis=0, concat_axis=0, tiled=True)  20.3 us
    all_to_all x1, waiting for transfers between devices, local(): lax.all_to_all(summed, 'ep', split_axis=0, concat_axis=0, tiled=True)  12 us
    all_to_all x1, starting transfers between devices, local(): lax.all_to_all(summed, 'ep', split_axis=0, concat_axis=0, tiled=True)  5.87 us
    dot_general x1, matrix products, local(): jnp.dot(active, down_weight[0], preferred_element_type=jnp.float32)  5.69 us
    reduce_scatter x1, waiting for transfers between devices, local(): lax.psum_scatter(partial_out, 'tp', scatter_dimension=1, tiled=True)  5.18 us
    dot_general x1, matrix products, local(): jnp.dot(flat_rows, gate_weight[0], preferred_element_type=jnp.float32)  2.68 us
    psum x1, blocking collectives, local(): logits = lax.psum(partial_logits, 'tp')  2.46 us
    all_gather x1, blocking collectives, local(): received = lax.all_gather(received, 'tp', axis=2, tiled=True)  2.45 us
  transfers between devices with their start and end apart: 2, of which 2 were waited for; matrix products, arithmetic and copies ran while one was open for 3% of the time, Pallas kernels for 0%

commit v1 on v0

--- a/solution.py
+++ b/solution.py
@@ -24,7 +24,7 @@
     expert_count = lax.axis_size("ep")
     capacity = min(token_count, 4 * token_count * top_count // expert_count)
     partial_logits = jnp.dot(hidden, router_weight, preferred_element_type=jnp.float32)
-    logits = lax.psum(partial_logits, "tp")
+    logits = jnp.sum(lax.all_gather(partial_logits, "tp"), axis=0)
     affinity = jax.nn.sigmoid(logits)
     expert_iota = jnp.arange(expert_count, dtype=jnp.int32)
     chosen_mask = routes[:, :, None] == expert_iota[None, None, :]

time: 80 us -> 80 us (level)
    psum x1 -> x0, blocking collectives: 2.46 us -> none  [local(): logits = lax.psum(partial_logits, 'tp')]
    all_gather x0 -> x1, blocking collectives: none -> 1.82 us  [local(): logits = jnp.sum(lax.all_gather(partial_logits, 'tp'), axis=0)]
where the time goes in v1:
time: 80 us; the launch traced here: 79.6 us
  blocking collectives  24.6 us (31%)
  waiting for transfers between devices  17.8 us (22%)
  between operations  14.2 us (18%)
  matrix products  11.2 us (14%)
  starting transfers between devices  5.91 us (7%)
  other arithmetic  3.88 us (5%)
  local copies, waits for them, and re-layouts  2.09 us (3%)
    all_to_all x1, blocking collectives, local(): lax.all_to_all(outgoing, 'ep', split_axis=0, concat_axis=0, tiled=True)  20.3 us
    all_to_all x1, waiting for transfers between devices, local(): lax.all_to_all(summed, 'ep', split_axis=0, concat_axis=0, tiled=True)  12 us
    all_to_all x1, starting transfers between devices, local(): lax.all_to_all(summed, 'ep', split_axis=0, concat_axis=0, tiled=True)  5.87 us
    reduce_scatter x1, waiting for transfers between devices, local(): lax.psum_scatter(partial_out, 'tp', scatter_dimension=1, tiled=True)  5.81 us
    dot_general x1, matrix products, local(): jnp.dot(active, down_weight[0], preferred_element_type=jnp.float32)  5.69 us
    dot_general x1, matrix products, local(): jnp.dot(flat_rows, gate_weight[0], preferred_element_type=jnp.float32)  2.68 us
    all_gather x1, blocking collectives, local(): received = lax.all_gather(received, 'tp', axis=2, tiled=True)  2.45 us
    convert_element_type x1, other arithmetic, local(): lax.psum_scatter(partial_out, 'tp', scatter_dimension=1, tiled=True)  2 us
  transfers between devices with their start and end apart: 2, of which 2 were waited for; matrix products, arithmetic and copies ran while one was open for 3% of the time, Pallas kernels for 0%

profile of v1, /device:TPU:0, one launch (start us, length us, event | category | flops | bytes accessed | tf_op | source)
XLA Modules:
  0.0 79.6 jit_solution(11592886174548873208)
XLA Ops:
  7.2 0.0 copy-start
  7.2 0.0 reduce-scatter.2.cloned.1.call-start
  7.2 0.8 %copy.24 = s32[16,4]{1,0:T(8,128)S(1)} copy(s32[16,4]{0,1:T(4,128)} %param.12) | data formatting | bytes 512 | tf_op args[1]
  8.1 0.1 eq.38
  8.2 0.1 fusion.27
  8.2 0.1 reduce_window_sum.11
  8.3 0.2 select_reduce_fusion
  8.5 0.1 reshape.114
  8.6 0.1 copy.26
  8.7 0.1 convert_reduce_fusion
  8.8 1.1 %convolution_convert_fusion = bf16[128,1792]{1,0:T(8,128)(2,1)S(1)} fusion(bf16[16,1792]{1,0:T(8,128)(2,1)} %param.11, s32[128,16]{0,1:T(8,128)S(1)} %convert_reduce_fusion), kind=kOutput, calls=%fused_computation.8 | convolution fusion | flops 7571456 | bytes 524288 | tf_op jit(solution)/shard_map/dot_general | solution.py:42
  9.9 20.3 %all_to_all.10 = bf16[8,16,1792]{2,1,0:T(8,128)(2,1)S(1)} all-to-all(bf16[8,16,1792]{2,1,0:T(8,128)(2,1)S(1)} %bitcast.38), channel_id=1, replica_groups=mesh['groups'=2,'ep'=8,'tp'=2] {'ep'}, dimensions={0} | all-to-all | bytes 917504 | tf_op jit(solution)/shard_map/all_to_all | solution.py:44
  30.2 2.5 %all_gather.11 = bf16[8,16,3584]{2,1,0:T(8,128)(2,1)S(1)} all-gather(bf16[8,16,1792]{2,1,0:T(8,128)(2,1)S(1)} %all_to_all.10), channel_id=1, replica_groups=mesh['groups'=2,'ep'=8,'tp'=2] {'tp'}, dimensions={2}, use_global_device_ids=true | all-gather | bytes 1376256 | tf_op jit(solution)/shard_map/all_gather | solution.py:45
  32.7 2.7 %fusion.5 = f32[128,512]{1,0:T(8,128)S(1)} fusion(bf16[128,3584]{1,0:T(8,128)(2,1)S(1)} %bitcast.36, bf16[1,3584,512]{2,1,0:T(8,128)(2,1)} %param.14), kind=kOutput, calls=%fused_computation.6 | convolution fusion | flops 469762048 | bytes 4849664 | tf_op jit(solution)/shard_map/dot_general | solution.py:48
  35.4 0.0 copy-start.1
  35.4 0.0 copy-start.5
  35.4 0.0 copy-start.6
  35.4 0.0 copy-start.2
  35.4 5.7 %fusion.1 = f32[128,3584]{1,0:T(8,128)} fusion(bf16[1,512,3584]{2,1,0:T(8,128)(2,1)} %param.16, bf16[128,3584]{1,0:T(8,128)(2,1)S(1)} %bitcast.37, bf16[1,3584,512]{2,1,0:T(8,128)(2,1)} %param.15, f32[128,512]{1,0:T(8,128)S(1)} %fusion.5), kind=kOutput, calls=%fused_computation.2 | convolution fusion | flops 939917312 | bytes 10354688 | tf_op jit(solution)/shard_map/dot_general | solution.py:51
  41.1 0.0 copy-start.7
  41.1 0.0 copy-start.3
  41.1 0.0 copy-start.4
  41.1 0.0 reduce-scatter.2.cloned.1.call-update
  41.1 0.1 reshape.119
  41.2 0.0 copy-done.1
  41.2 0.0 copy-done.5
  41.2 0.1 convolution_bitcast_fusion
  41.3 1.8 %all-gather.1 = f32[2,16,8]{1,2,0:T(8,128)S(1)} all-gather(f32[1,16,8]{1,2,0:T(8,128)S(1)} %convolution_bitcast_fusion), channel_id=2, replica_groups=mesh['groups'=2,'ep'=8,'tp'=2] {'tp'}, dimensions={0}, use_global_device_ids=true | all-gather | bytes 1536 | tf_op jit(solution)/shard_map/all_gather | solution.py:27
  43.2 0.0 copy-done.6
  43.2 0.1 copy.23
  43.3 0.0 copy-done
  43.3 0.0 copy-done.2
  43.3 0.4 fusion.34
  43.8 5.8 %reduce-scatter.2.cloned.1.call-done = f32[128,1792]{1,0:T(8,128)} async-done(((f32[128,3584]{1,0:T(8,128)}), f32[128,1792]{1,0:T(8,128)}) %reduce-scatter.2.cloned.1.call-update) | async-done | bytes 917520 | tf_op jit(solution)/shard_map/reduce_scatter | solution.py:52
  49.6 2.0 %convert_element_type.35 = bf16[128,1792]{1,0:T(8,128)(2,1)} convert(f32[128,1792]{1,0:T(8,128)} %reduce-scatter.2.cloned.1.call-done) | non-fusion elementwise | flops 229376 | bytes 1376256 | tf_op jit(solution)/shard_map/convert_element_type | solution.py:52
  51.6 5.9 %all-to-all-start.1 = ((bf16[8,16,1792]{2,1,0:T(8,128)(2,1)}), bf16[8,16,1792]{2,1,0:T(8,128)(2,1)S(1)}, u32[]{:S(2)}, u32[]{:S(2)}) async-start(bf16[8,16,1792]{2,1,0:T(8,128)(2,1)} %bitcast.6), calls=%async_computation.2 | async-start | bytes 917504 | tf_op jit(solution)/shard_map/all_to_all | solution.py:56
  57.4 0.0 copy-done.7
  57.4 0.1 iota_compare_fusion.3
  57.5 0.0 copy-done.3
  57.5 0.0 copy-done.4
  57.5 0.2 fusion.17
  57.7 0.2 fusion.33
  57.9 1.0 %convolution_convert_fusion.1 = bf16[4,32,512]{2,1,0:T(8,128)(2,1)} fusion(bf16[4,256,512]{2,1,0:T(8,128)(2,1)S(1)} %copy-done, f32[4,32]{1,0:T(4,128)S(1)} %fusion.33, f32[4,32,256]{2,1,0:T(8,128)S(1)} %fusion.17, pred[4,256]{1,0:T(4,128)(4,1)S(1)} %iota_compare_fusion.3), kind=kOutput, calls=%fused_computation.11 | convolution fusion | flops 33751424 | bytes 1312256 | tf_op jit(solution)/shard_map/bhj,bjl->bhl/dot_general | solution.py:68
  58.8 12.0 %all-to-all-done.1 = bf16[8,16,1792]{2,1,0:T(8,128)(2,1)S(1)} async-done(((bf16[8,16,1792]{2,1,0:T(8,128)(2,1)}), bf16[8,16,1792]{2,1,0:T(8,128)(2,1)S(1)}, u32[]{:S(2)}, u32[]{:S(2)}) %all-to-all-start.1) | async-done | bytes 458784 | tf_op jit(solution)/shard_map/all_to_all | solution.py:56
  70.8 0.7 gather_fusion
  71.6 0.1 gather.7
  71.7 1.1 %multiply_reduce_fusion = bf16[16,1792]{1,0:T(8,128)(2,1)} fusion(bf16[16,4,1792]{2,1,0:T(4,128)(2,1)S(1)} %gather.7, f32[16,4]{1,0:T(8,128)S(1)} %copy.23, pred[16,4]{1,0:T(8,128)(4,1)S(1)} %get-tuple-element.4), kind=kLoop, calls=%fused_computation.19 | loop fusion | flops 430080 | bytes 287040 | tf_op jit(solution)/shard_map/reduce_sum | solution.py:76
  (7 shorter events, 0.1 us)
Async XLA Ops:
  7.2 36.2 %copy-start = (bf16[4,256,512]{2,1,0:T(8,128)(2,1)S(1)}, bf16[4,256,512]{2,1,0:T(8,128)(2,1)}, u32[]{:S(2)}) copy-start(bf16[4,256,512]{2,1,0:T(8,128)(2,1)} %param.19) | copy-start | bytes 3145732
  7.2 42.4 %reduce-scatter.2.cloned.1.call-start = ((), (), s32[]{:S(2)}) async-start(), calls=%async_computation.3 | async-start | bytes 2752512 | tf_op jit(solution)/shard_map/reduce_scatter | solution.py:52
  35.4 5.9 %copy-start.1 = (bf16[16,1792]{1,0:T(8,128)(2,1)S(1)}, bf16[16,1792]{1,0:T(8,128)(2,1)}, u32[]{:S(2)}) copy-start(bf16[16,1792]{1,0:T(8,128)(2,1)} %param.11) | copy-start | bytes 172036
  35.4 5.9 %copy-start.5 = (bf16[1792,8]{0,1:T(8,128)(2,1)S(1)}, bf16[1792,8]{0,1:T(8,128)(2,1)}, u32[]{:S(2)}) copy-start(bf16[1792,8]{0,1:T(8,128)(2,1)} %param.13) | copy-start | bytes 86020
  35.4 7.8 %copy-start.6 = (s32[16,4]{0,1:T(4,128)S(1)}, s32[16,4]{0,1:T(4,128)}, u32[]{:S(2)}) copy-start(s32[16,4]{0,1:T(4,128)} %param.12) | copy-start | bytes 772
  35.4 8.0 %copy-start.2 = (bf16[4,32,512]{2,1,0:T(8,128)(2,1)S(1)}, bf16[4,32,512]{2,1,0:T(8,128)(2,1)}, u32[]{:S(2)}) copy-start(bf16[4,32,512]{2,1,0:T(8,128)(2,1)} %param.17) | copy-start | bytes 393220
  41.1 16.3 %copy-start.7 = (s32[4]{0:T(128)S(1)}, s32[4]{0:T(128)}, u32[]{:S(2)}) copy-start(s32[4]{0:T(128)} %param.21) | copy-start | bytes 52
  41.1 16.4 %copy-start.3 = (bf16[4,64,256]{2,1,0:T(8,128)(2,1)S(1)}, bf16[4,64,256]{2,1,0:T(8,128)(2,1)}, u32[]{:S(2)}) copy-start(bf16[4,64,256]{2,1,0:T(8,128)(2,1)} %param.20) | copy-start | bytes 393220
  41.1 16.4 %copy-start.4 = (bf16[4,32,64]{2,1,0:T(8,128)(2,1)S(1)}, bf16[4,32,64]{2,1,0:T(8,128)(2,1)}, u32[]{:S(2)}) copy-start(bf16[4,32,64]{2,1,0:T(8,128)(2,1)} %param.18) | copy-start | bytes 49156
  51.6 19.3 %all-to-all-start.1 = ((bf16[8,16,1792]{2,1,0:T(8,128)(2,1)}), bf16[8,16,1792]{2,1,0:T(8,128)(2,1)S(1)}, u32[]{:S(2)}, u32[]{:S(2)}) async-start(bf16[8,16,1792]{2,1,0:T(8,128)(2,1)} %bitcast.6), calls=%async_computation.2 | async-start | bytes 917504 | tf_op jit(solution)/shard_map/all_to_all | solution.py:56
Sparse Core Ops, SparseCore 0:
  41.2 8.2 reduce-scatter.1
